TPU v7x, 128 devices: a whole 4x4x4 slice. The times are simulated.
128 devices in a mesh: slab: 8 (over z, core), tile: 16 (over x, y).
Axes of the slice: x: 4, y: 4, z: 4, core: 2. Of those that a mesh axis runs over, the one named last changes fastest.
Arguments:
- coarse: bfloat16 [192, 32, 64, 64], P(None, 'slab', 'tile'), may hold values from -6 to 6
- up_weight: bfloat16 [3, 3, 96, 192], replicated, may hold values from -0.15625 to 0.15625
- up_bias: float32 [96], replicated, may hold values from -3 to 3
- gain_one: float32 [96], replicated, may hold values from 0.1 to 1.9
- conv_one: bfloat16 [3, 3, 96, 288], replicated, may hold values from -0.125 to 0.125
- bias_one: float32 [96], replicated, may hold values from -3 to 3
- gain_two: float32 [96], replicated, may hold values from 0.1 to 1.9
- conv_two: bfloat16 [3, 3, 96, 288], replicated, may hold values from -0.125 to 0.125
- bias_two: float32 [96], replicated, may hold values from -3 to 3
Outputs:
- decoded: bfloat16 [96, 32, 128, 128], P(None, 'slab', 'tile')
All inputs are finite; a program needn't handle non-finite values.
Results may differ from a plain program's by a relative error of at most 0.009.
Values may be sent and summed in bfloat16 or wider, within the bound.
No kernel may reach another device: no remote copies, remote signals or barrier semaphores. Data moves between devices by JAX's collectives and lax.ppermute only.
A program may use at most 64 MiB of HBM per device.

v0:
```python
import jax
import jax.numpy as jnp
import numpy as np
from jax import lax
from jax.experimental import pallas as pl
from jax.experimental.pallas import tpu as pltpu
from jax.sharding import PartitionSpec as P

F32 = jnp.float32
BF16 = jnp.bfloat16
CH = 96


def silu(y):
    return y * (0.5 + 0.5 * jnp.tanh(0.5 * y))


def norm_act(v, gain):
    meansq = jnp.sum(v * v, axis=0, keepdims=True) * (1.0 / CH)
    return silu(v * lax.rsqrt(meansq + 1e-06) * gain)


def lanes_of(shape):
    return lax.broadcasted_iota(jnp.int32, shape, 1)


def spread_matrix():
    m = np.zeros((256, 256), np.float32)
    for q in range(2):
        for f in range(2):
            for j in range(64):
                m[q * 128 + f * 64 + j, f * 128 + 2 * j + q] = 1
    return m


def up_stage(x_ref, wup_ref, spread_ref, bias_ref, gain_ref, act_ref, first, raw_ref, valid):
    low = lanes_of((CH, 128)) % 64 == 0
    high = lanes_of((CH, 128)) % 64 == 63

    def row(i, carry):
        for p in range(2):
            top = x_ref[:, i + p].reshape(256, 192)
            bottom = x_ref[:, i + p + 1].reshape(256, 192)
            dims = (((1,), (1,)), ((), ()))
            u = lax.dot_general(wup_ref[2 * p], top, dims, preferred_element_type=F32)
            u = u + lax.dot_general(wup_ref[2 * p + 1], bottom, dims, preferred_element_type=F32)
            stacked = []
            for g in range(2):
                part = u[:, 128 * g:128 * g + 128]
                even = part[:CH] + jnp.where(low, 0.0, pltpu.roll(part[CH:2 * CH], 1, 1)) + bias_ref[...]
                odd = part[2 * CH:3 * CH] + jnp.where(high, 0.0, pltpu.roll(part[3 * CH:], 127, 1)) + bias_ref[...]
                stacked.append(jnp.concatenate([even.astype(BF16), odd.astype(BF16)], axis=1))
            fine = jnp.dot(jnp.concatenate(stacked, axis=0), spread_ref[...], preferred_element_type=F32)
            for g in range(2):
                for h in range(2):
                    v = fine[CH * g:CH * g + CH, 128 * h:128 * h + 128]
                    if raw_ref is not None:
                        raw_ref[2 * g + h, 2 * i + p] = v.astype(BF16)
                    act = jnp.where(valid(i), norm_act(v, gain_ref[...]), 0.0)
                    act_ref[first + 2 * g + h, 2 * i + p] = act.astype(BF16)
        return carry

    lax.fori_loop(0, 6, row, 0)


def conv_pair(src_ref, w_ref, f, r):
    taps = [
        jnp.concatenate([src_ref[f + t, r + a], src_ref[f + t, r + a + 1]], axis=1)
        for t in range(3) for a in range(3)
    ]
    s = jnp.dot(w_ref[...], jnp.concatenate(taps, axis=0), preferred_element_type=F32)
    lane = lanes_of((CH, 128))
    rows = []
    for h in range(2):
        part = s[:, 128 * h:128 * h + 128]
        left = jnp.where(lane == 0, 0.0, pltpu.roll(part[:CH], 1, 1))
        right = jnp.where(lane == 127, 0.0, pltpu.roll(part[2 * CH:], 127, 1))
        rows.append(left + part[CH:2 * CH] + right)
    return rows


def conv_one_stage(act_ref, w_ref, bias_ref, gain_ref, hid_ref, low, high, valid):
    def frame(f, carry):
        for pair in range(5):
            rows = conv_pair(act_ref, w_ref, f, 2 * pair)
            for h in range(2):
                q = 2 * pair + h
                act = norm_act(rows[h] + bias_ref[...], gain_ref[...])
                act = jnp.where(valid(f, q), act, 0.0)
                hid_ref[f, q] = act.astype(BF16)
        return carry

    lax.fori_loop(low, high, frame, 0)


def conv_two_stage(hid_ref, w_ref, bias_ref, raw_ref, out_ref, mix_ref):
    def frame(f, carry):
        for pair in range(4):
            rows = conv_pair(hid_ref, w_ref, f, 2 * pair)
            for h in range(2):
                r = 2 * pair + h
                res = raw_ref[f, r + 2].astype(F32) + rows[h] + bias_ref[...]
                mix_ref[pl.ds(r, CH, stride=8), :] = res
        out_ref[:, f] = mix_ref[...].reshape(CH, 8, 128).astype(BF16)
        return carry

    lax.fori_loop(0, 4, frame, 0)


def whole_kernel(flags, own_ref, old_ref, wup_ref, spread_ref, upb_ref, g1_ref, w1_ref, b1_ref, g2_ref, w2_ref, b2_ref,
                 out_ref, act_ref, hid_ref, raw_ref, mix_ref):
    has_top, has_bottom, has_old = flags[0] > 0, flags[1] > 0, flags[2] > 0

    def in_image(i, last):
        return jnp.logical_and(jnp.logical_or(i > 0, has_top), jnp.logical_or(i < last, has_bottom))

    up_stage(own_ref, wup_ref, spread_ref, upb_ref, g1_ref, act_ref, 4, raw_ref, lambda i: in_image(i, 5))
    up_stage(old_ref, wup_ref, spread_ref, upb_ref, g1_ref, act_ref, 0, None,
             lambda i: jnp.logical_and(in_image(i, 5), has_old))

    def hidden_valid(f, q):
        ok = jnp.logical_or(f >= 2, has_old)
        if q == 0:
            ok = jnp.logical_and(ok, has_top)
        if q == 9:
            ok = jnp.logical_and(ok, has_bottom)
        return ok

    conv_one_stage(act_ref, w1_ref, b1_ref, g2_ref, hid_ref, 0, 6, hidden_valid)
    conv_two_stage(hid_ref, w2_ref, b2_ref, raw_ref, out_ref, mix_ref)


def up_weights(w):
    w = w.astype(F32)
    rows = [w[0], w[1] + w[2], w[0] + w[1], w[2]]
    return jnp.stack([
        jnp.concatenate([r[1] + r[2], r[0], r[0] + r[1], r[2]], axis=0) for r in rows
    ]).astype(BF16)


def conv_weights(w):
    return w.reshape(3, 3, CH, 3, CH).transpose(3, 2, 0, 1, 4).reshape(3 * CH, 9 * CH)


def column(v):
    return jnp.broadcast_to(v[:, None], (CH, 128))


def shards(coarse, up_weight, up_bias, gain_one, conv_one, bias_one, gain_two, conv_two, bias_two):
    tiles, slabs = lax.axis_size("tile"), lax.axis_size("slab")
    x = coarse.transpose(1, 2, 3, 0)
    above = lax.ppermute(x[:, 2:], "tile", [(i, i + 1) for i in range(tiles - 1)])
    below = lax.ppermute(x[:, :2], "tile", [(i + 1, i) for i in range(tiles - 1)])
    own = jnp.concatenate([above, x, below], axis=1)
    old = lax.ppermute(own, "slab", [(i, i + 1) for i in range(slabs - 1)])
    place, age = lax.axis_index("tile"), lax.axis_index("slab")
    flags = jnp.stack([place, tiles - 1 - place, age]).astype(jnp.int32)
    vmem = pl.BlockSpec(memory_space=pltpu.VMEM)
    return pl.pallas_call(
        whole_kernel,
        out_shape=jax.ShapeDtypeStruct((CH, 4, 8, 128), BF16),
        in_specs=[pl.BlockSpec(memory_space=pltpu.SMEM)] + [vmem] * 11,
        out_specs=vmem,
        scratch_shapes=[
            pltpu.VMEM((8, 12, CH, 128), BF16),
            pltpu.VMEM((6, 10, CH, 128), BF16),
            pltpu.VMEM((4, 12, CH, 128), BF16),
            pltpu.VMEM((CH * 8, 128), F32),
        ],
        compiler_params=pltpu.CompilerParams(vmem_limit_bytes=48 << 20),
        name="decode",
    )(flags, own, old, up_weights(up_weight), jnp.asarray(spread_matrix(), BF16), column(up_bias), column(gain_one),
      conv_weights(conv_one), column(bias_one), column(gain_two), conv_weights(conv_two), column(bias_two))


def solution(mesh):
    return jax.shard_map(
        shards,
        mesh=mesh,
        in_specs=(P(None, "slab", "tile", None), P(), P(), P(), P(), P(), P(), P(), P()),
        out_specs=P(None, "slab", "tile", None),
        check_vma=False,
    )
```

profile of v0, /device:TPU:56, one launch (start us, length us, event | category | flops | bytes accessed | tf_op | source)
XLA Modules:
  0.0 61.1 jit_solution(1069484179230383044)
XLA Ops:
  0.0 1.9 %fusion.16 = (bf16[4,2,64,192]{3,2,1,0:T(8,128)(2,1)}, bf16[4,2,64,192]{3,2,1,0:T(8,128)(2,1)}) fusion(bf16[4,4,64,192]{3,2,1,0:T(8,128)(2,1)} %bitcast.52), kind=kLoop, calls=%fused_computation.41 | loop fusion | bytes 786432 | tf_op jit(solution)/shard_map/slice | solution.py:152
  1.9 3.0 %collective-permute-start = (bf16[4,2,64,192]{3,2,1,0:T(8,128)(2,1)}, bf16[4,2,64,192]{3,2,1,0:T(8,128)(2,1)}, u32[]{:S(2)}, u32[]{:S(2)}) collective-permute-start(bf16[4,2,64,192]{3,2,1,0:T(8,128)(2,1)} %get-tuple-element.15), channel_id=1, source_target_pairs={{0,1},{1,2},{2,3},{3,4},{4,5},{5,6},{6,7},{7,8},{8,9},{9,10},{10,1... | collective-permute-start | bytes 589832 | tf_op jit(solution)/shard_map/ppermute | solution.py:152
  5.0 2.8 %collective-permute-start.1 = (bf16[4,2,64,192]{3,2,1,0:T(8,128)(2,1)}, bf16[4,2,64,192]{3,2,1,0:T(8,128)(2,1)}, u32[]{:S(2)}, u32[]{:S(2)}) collective-permute-start(bf16[4,2,64,192]{3,2,1,0:T(8,128)(2,1)} %get-tuple-element.16), channel_id=1, source_target_pairs={{1,0},{2,1},{3,2},{4,3},{5,4},{6,5},{7,6},{8,7},{9,8},{10,9},{11,1... | collective-permute-start | bytes 589832 | tf_op jit(solution)/shard_map/ppermute | solution.py:153
  7.8 0.1 convert_element_type.4
  7.9 0.1 slice_add_fusion.1
  7.9 0.7 %fusion.3 = (bf16[96,192]{1,0:T(8,128)(2,1)}, bf16[96,192]{1,0:T(8,128)(2,1)}, bf16[96,192]{1,0:T(8,128)(2,1)S(1)}, bf16[96,192]{1,0:T(8,128)(2,1)}) fusion(f32[1,3,96,192]{3,2,1,0:T(8,128)S(1)} %get-tuple-element.13, f32[1,3,96,192]{3,2,1,0:T(8,128)S(1)} %get-tuple-element.14), kind=kLoop, calls=%fused_computation.27 | loop fusion | bytes 294912 | tf_op jit(solution)/shard_map/convert.16
  8.6 0.7 %fusion.10 = (bf16[96,192]{1,0:T(8,128)(2,1)}, bf16[96,192]{1,0:T(8,128)(2,1)}, bf16[96,192]{1,0:T(8,128)(2,1)}, bf16[96,192]{1,0:T(8,128)(2,1)}) fusion(f32[1,3,96,192]{3,2,1,0:T(8,128)S(1)} %get-tuple-element.13, f32[1,3,96,192]{3,2,1,0:T(8,128)S(1)} %get-tuple-element.14), kind=kLoop, calls=%fused_computation.34 | loop fusion | flops 147456 | bytes 589824 | tf_op jit(solution)/shard_map/convert.15
  9.3 0.4 copy.13
  9.7 0.7 %copy.14 = bf16[3,96,3,3,96]{4,3,2,1,0:T(4,128)(2,1)S(1)} copy(bf16[3,96,3,3,96]{1,4,0,3,2:T(8,128)(2,1)S(1)} %bitcast.50) | data formatting | bytes 995328 | tf_op jit(solution)/shard_map/transpose | solution.py:142
  10.3 0.6 reshape.44.w1_ref
  11.0 1.4 %copy.15 = bf16[3,3,96,288]{2,3,1,0:T(8,128)(2,1)S(1)} copy(bf16[3,3,96,288]{3,2,1,0:T(8,128)(2,1)} %param.17) | data formatting | bytes 995328 | tf_op args[7]
  12.4 0.7 %copy.16 = bf16[3,96,3,3,96]{4,3,2,1,0:T(4,128)(2,1)S(1)} copy(bf16[3,96,3,3,96]{1,4,0,3,2:T(8,128)(2,1)S(1)} %bitcast.51) | data formatting | bytes 995328 | tf_op jit(solution)/shard_map/transpose | solution.py:142
  13.1 0.6 reshape.46.w2_ref
  13.7 1.0 %maximum_bitcast_fusion.1 = bf16[1,384,192]{2,1,0:T(8,128)(2,1)S(1)} fusion(bf16[96,192]{1,0:T(8,128)(2,1)} %get-tuple-element.20, bf16[96,192]{1,0:T(8,128)(2,1)} %get-tuple-element.18, bf16[96,192]{1,0:T(8,128)(2,1)} %get-tuple-element.19, bf16[96,192]{1,0:T(8,128)(2,1)} %get-tuple-element.17), kind=kLoop, calls=%fused_computation.5 | loop fusion | flops 589824 | bytes 294912 | tf_op jit(solution)/shard_map/stack | solution.py:136
  14.7 0.8 %maximum_bitcast_fusion.2 = bf16[1,384,192]{2,1,0:T(8,128)(2,1)S(1)} fusion(bf16[96,192]{1,0:T(8,128)(2,1)S(1)} %get-tuple-element.27, bf16[96,192]{1,0:T(8,128)(2,1)S(1)} %copy-done.5, bf16[96,192]{1,0:T(8,128)(2,1)S(1)} %copy-done.4, bf16[96,192]{1,0:T(8,128)(2,1)} %get-tuple-element.30), kind=kLoop, calls=%fused_computation.6 | loop fusion | flops 589824 | bytes 294912 | tf_op jit(solution)/shard_map/stack | solution.py:136
  15.5 1.5 %collective-permute-done.1 = bf16[4,2,64,192]{3,2,1,0:T(8,128)(2,1)} collective-permute-done((bf16[4,2,64,192]{3,2,1,0:T(8,128)(2,1)}, bf16[4,2,64,192]{3,2,1,0:T(8,128)(2,1)}, u32[]{:S(2)}, u32[]{:S(2)}) %collective-permute-start.1) | collective-permute-done | bytes 196640 | tf_op jit(solution)/shard_map/ppermute | solution.py:153
  17.1 1.2 %pad_maximum_fusion.own_ref = bf16[4,8,64,192]{3,2,1,0:T(8,128)(2,1)S(1)} fusion(bf16[4,2,64,192]{3,2,1,0:T(8,128)(2,1)} %collective-permute-done.1, bf16[4,4,64,192]{3,2,1,0:T(8,128)(2,1)S(1)} %bitcast.53, bf16[4,2,64,192]{3,2,1,0:T(8,128)(2,1)} %collective-permute-done), kind=kLoop, calls=%fused_computation | loop fusion | flops 786432 | bytes 1572864 | tf_op jit(solution)/shard_map/concatenate | solution.py:154
  18.3 1.9 %collective-permute-start.2 = (bf16[4,8,64,192]{3,2,1,0:T(8,128)(2,1)S(1)}, bf16[4,8,64,192]{3,2,1,0:T(8,128)(2,1)S(1)}, u32[]{:S(2)}, u32[]{:S(2)}) collective-permute-start(bf16[4,8,64,192]{3,2,1,0:T(8,128)(2,1)S(1)} %pad_maximum_fusion.own_ref), channel_id=1, source_target_pairs={{0,16},{16,32},{32,48},{48,64},{64,80},{80,96},{96,112},{1,17},{17... | collective-permute-start | bytes 2359304 | tf_op jit(solution)/shard_map/ppermute | solution.py:155
  20.2 0.1 pad_add_fusion.flags
  20.4 0.1 maximum_bitcast_fusion
  20.5 0.2 pad_maximum_fusion.1.wup_ref
  20.7 0.0 copy-start
  20.7 13.7 %collective-permute-done.2.old_ref = bf16[4,8,64,192]{3,2,1,0:T(8,128)(2,1)S(1)} collective-permute-done((bf16[4,8,64,192]{3,2,1,0:T(8,128)(2,1)S(1)}, bf16[4,8,64,192]{3,2,1,0:T(8,128)(2,1)S(1)}, u32[]{:S(2)}, u32[]{:S(2)}) %collective-permute-start.2) | collective-permute-done | bytes 786464 | tf_op jit(solution)/shard_map/ppermute | solution.py:155
  34.4 0.1 broadcast_in_dim.10.upb_ref
  34.5 0.1 broadcast_in_dim.11.g1_ref
  34.6 0.0 copy-start.9
  34.6 0.1 broadcast_in_dim.12.b1_ref
  34.7 0.6 copy-done.9
  35.2 0.1 broadcast_in_dim.13.g2_ref
  35.3 0.6 copy-done.10
  35.9 0.1 broadcast_in_dim.14.b2_ref
  36.0 25.2 %decode.1 = bf16[96,4,8,128]{3,2,1,0:T(8,128)(2,1)} custom-call(s32[3]{0:T(128)S(1)} %pad_add_fusion.flags, bf16[4,8,64,192]{3,2,1,0:T(8,128)(2,1)S(1)} %pad_maximum_fusion.own_ref, bf16[4,8,64,192]{3,2,1,0:T(8,128)(2,1)S(1)} %collective-permute-done.2.old_ref, bf16[4,384,192]{2,1,0:T(8,128)(2,1)S(1)} %pad_maximum_fusion.1.wup_ref, ...), custom_call_target="tpu_custom_call" | custom-call | tf_op jit(solution)/shard_map/decode/pallas_call | solution.py:159
  (21 shorter events, 0.1 us)
Async XLA Ops:
  0.0 7.8 %copy-start.3 = (bf16[3,3,96,192]{3,2,1,0:T(8,128)(2,1)S(1)}, bf16[3,3,96,192]{3,2,1,0:T(8,128)(2,1)}, u32[]{:S(2)}) copy-start(bf16[3,3,96,192]{3,2,1,0:T(8,128)(2,1)} %param.11) | copy-start | bytes 995332
  1.9 13.6 %collective-permute-start = (bf16[4,2,64,192]{3,2,1,0:T(8,128)(2,1)}, bf16[4,2,64,192]{3,2,1,0:T(8,128)(2,1)}, u32[]{:S(2)}, u32[]{:S(2)}) collective-permute-start(bf16[4,2,64,192]{3,2,1,0:T(8,128)(2,1)} %get-tuple-element.15), channel_id=1, source_target_pairs={{0,1},{1,2},{2,3},{3,4},{4,5},{5,6},{6,7},{7,8},{8,9},{9,10},{10,1... | collective-permute-start | bytes 589832 | tf_op jit(solution)/shard_map/ppermute | solution.py:152
  5.0 12.1 %collective-permute-start.1 = (bf16[4,2,64,192]{3,2,1,0:T(8,128)(2,1)}, bf16[4,2,64,192]{3,2,1,0:T(8,128)(2,1)}, u32[]{:S(2)}, u32[]{:S(2)}) collective-permute-start(bf16[4,2,64,192]{3,2,1,0:T(8,128)(2,1)} %get-tuple-element.16), channel_id=1, source_target_pairs={{1,0},{2,1},{3,2},{4,3},{5,4},{6,5},{7,6},{8,7},{9,8},{10,9},{11,1... | collective-permute-start | bytes 589832 | tf_op jit(solution)/shard_map/ppermute | solution.py:153
  7.9 1.4 %copy-start.2 = (bf16[3,3,96,288]{3,2,1,0:T(8,128)(2,1)S(1)}, bf16[3,3,96,288]{3,2,1,0:T(8,128)(2,1)}, u32[]{:S(2)}) copy-start(bf16[3,3,96,288]{3,2,1,0:T(8,128)(2,1)} %param.14) | copy-start | bytes 1492996
  13.1 1.6 %copy-start.4 = (bf16[96,192]{1,0:T(8,128)(2,1)S(1)}, bf16[96,192]{1,0:T(8,128)(2,1)}, u32[]{:S(2)}) copy-start(bf16[96,192]{1,0:T(8,128)(2,1)} %get-tuple-element.28) | copy-start | bytes 110596
  13.1 1.6 %copy-start.5 = (bf16[96,192]{1,0:T(8,128)(2,1)S(1)}, bf16[96,192]{1,0:T(8,128)(2,1)}, u32[]{:S(2)}) copy-start(bf16[96,192]{1,0:T(8,128)(2,1)} %get-tuple-element.29) | copy-start | bytes 110596
  13.7 3.4 %copy-start.1 = (bf16[192,4,4,64]{0,3,2,1:T(8,128)(2,1)S(1)}, bf16[192,4,4,64]{0,3,2,1:T(8,128)(2,1)}, u32[]{:S(2)}) copy-start(bf16[192,4,4,64]{0,3,2,1:T(8,128)(2,1)} %param.10) | copy-start | bytes 1179652
  18.3 16.1 %collective-permute-start.2 = (bf16[4,8,64,192]{3,2,1,0:T(8,128)(2,1)S(1)}, bf16[4,8,64,192]{3,2,1,0:T(8,128)(2,1)S(1)}, u32[]{:S(2)}, u32[]{:S(2)}) collective-permute-start(bf16[4,8,64,192]{3,2,1,0:T(8,128)(2,1)S(1)} %pad_maximum_fusion.own_ref), channel_id=1, source_target_pairs={{0,16},{16,32},{32,48},{48,64},{64,80},{80,96},{96,112},{1,17},{17... | collective-permute-start | bytes 2359304 | tf_op jit(solution)/shard_map/ppermute | solution.py:155
  20.5 14.0 %copy-start.6 = (f32[96]{0:T(128)S(1)}, f32[96]{0:T(128)}, u32[]{:S(2)}) copy-start(f32[96]{0:T(128)} %param.12) | copy-start | bytes 1156
  20.5 14.0 %copy-start.7 = (f32[96]{0:T(128)S(1)}, f32[96]{0:T(128)}, u32[]{:S(2)}) copy-start(f32[96]{0:T(128)} %param.13) | copy-start | bytes 1156
  20.5 14.1 %copy-start.8 = (f32[96]{0:T(128)S(1)}, f32[96]{0:T(128)}, u32[]{:S(2)}) copy-start(f32[96]{0:T(128)} %param.15) | copy-start | bytes 1156
  20.7 15.3 %copy-start = (bf16[256,256]{1,0:T(8,128)(2,1)S(1)}, bf16[256,256]{1,0:T(8,128)(2,1)}, u32[]{:S(2)}) copy-start(bf16[256,256]{1,0:T(8,128)(2,1)} %constant.13.clone.spread_ref) | copy-start | bytes 393220
  34.6 0.7 %copy-start.9 = (f32[96]{0:T(128)S(1)}, f32[96]{0:T(128)}, u32[]{:S(2)}) copy-start(f32[96]{0:T(128)} %param.16) | copy-start | bytes 1156
  35.2 0.7 %copy-start.10 = (f32[96]{0:T(128)S(1)}, f32[96]{0:T(128)}, u32[]{:S(2)}) copy-start(f32[96]{0:T(128)} %param.18) | copy-start | bytes 1156
where the time goes:
time: 62.1 us; the launch traced here: 61.1 us
  Pallas kernels  25.2 us (41%)
  waiting for transfers between devices  15.2 us (24%)
  local copies, waits for them, and re-layouts  8.52 us (14%)
  starting transfers between devices  7.75 us (12%)
  other arithmetic  4.23 us (7%)
    pallas_call x1, Pallas kernels, shards(): pl.pallas_call(whole_kernel, out_shape=jax.ShapeDtypeStruct((CH, 4, 8, 12...  25.2 us
    ppermute x1, waiting for transfers between devices, shards(): old = lax.ppermute(own, 'slab', [(i, i + 1) for i in range(slabs - 1)])  13.7 us
    ppermute x1, starting transfers between devices, shards(): lax.ppermute(x[:, 2:], 'tile', [(i, i + 1) for i in range(tiles - 1)])  3.05 us
    unnamed x24, local copies, waits for them, and re-layouts  3.04 us
    ppermute x1, starting transfers between devices, shards(): lax.ppermute(x[:, :2], 'tile', [(i + 1, i) for i in range(tiles - 1)])  2.79 us
    another operation x4, other arithmetic, up_weights(): jnp.stack([jnp.concatenate([r[1] + r[2], r[0], r[0] + r[1], r[2]], axis=0...  2.05 us
    ppermute x1, starting transfers between devices, shards(): old = lax.ppermute(own, 'slab', [(i, i + 1) for i in range(slabs - 1)])  1.92 us
    slice x1, local copies, waits for them, and re-layouts, shards(): x[:, 2:]  1.92 us
  transfers between devices with their start and end apart: 3, of which 2 were waited for; matrix products, arithmetic and copies ran while one was open for 13% of the time, Pallas kernels for 0%

commit v1 on v0

v1 whole, which is shorter than its diff:
```python
import jax
import jax.numpy as jnp
import numpy as np
from jax import lax
from jax.experimental import pallas as pl
from jax.experimental.pallas import tpu as pltpu
from jax.sharding import PartitionSpec as P

F32 = jnp.float32
BF16 = jnp.bfloat16
CH = 96
VMEM = pl.BlockSpec(memory_space=pltpu.VMEM)
SMEM = pl.BlockSpec(memory_space=pltpu.SMEM)
ANY = pl.BlockSpec(memory_space=pl.ANY)


def silu(y):
    return y * (0.5 + 0.5 * jnp.tanh(0.5 * y))


def norm_act(v, gain):
    meansq = jnp.sum(v * v, axis=0, keepdims=True) * (1.0 / CH)
    return silu(v * lax.rsqrt(meansq + 1e-06) * gain)


def lanes_of(shape):
    return lax.broadcasted_iota(jnp.int32, shape, 1)


def spread_matrix():
    m = np.zeros((256, 256), np.float32)
    for q in range(2):
        for f in range(2):
            for j in range(64):
                m[q * 128 + f * 64 + j, f * 128 + 2 * j + q] = 1
    return m


def prep_kernel(up_ref, one_ref, two_ref, upb_ref, g1_ref, b1_ref, g2_ref, b2_ref, wup_ref, w1_ref, w2_ref, cols_ref):
    for n in range(4):
        taps = []
        for b in range(3):
            if n == 0:
                tap = up_ref[0, b].astype(F32)
            elif n == 3:
                tap = up_ref[2, b].astype(F32)
            else:
                tap = up_ref[1, b].astype(F32) + up_ref[2 if n == 1 else 0, b].astype(F32)
            taps.append(tap)
        for m, tap in enumerate((taps[1] + taps[2], taps[0], taps[0] + taps[1], taps[2])):
            wup_ref[n, CH * m:CH * m + CH, :] = tap.astype(BF16)
    for src_ref, dst_ref in ((one_ref, w1_ref), (two_ref, w2_ref)):
        for b in range(3):
            pieces = [src_ref[t, a][:, CH * b:CH * b + CH] for t in range(3) for a in range(3)]
            dst_ref[CH * b:CH * b + CH, :] = jnp.concatenate(pieces, axis=1)
    for n, ref in enumerate((upb_ref, g1_ref, b1_ref, g2_ref, b2_ref)):
        cols_ref[n] = jnp.broadcast_to(ref[...], (128, CH)).T


def up_tile(blocks, p, x_ref, wup_ref, spread_ref, bias, gain, emit):
    low = lanes_of((CH, 128)) % 64 == 0
    high = lanes_of((CH, 128)) % 64 == 63
    dims = (((1,), (1,)), ((), ()))
    u = lax.dot_general(wup_ref[2 * p], blocks(p), dims, preferred_element_type=F32)
    u = u + lax.dot_general(wup_ref[2 * p + 1], blocks(p + 1), dims, preferred_element_type=F32)
    stacked = []
    for g in range(2):
        part = u[:, 128 * g:128 * g + 128]
        even = part[:CH] + jnp.where(low, 0.0, pltpu.roll(part[CH:2 * CH], 1, 1)) + bias
        odd = part[2 * CH:3 * CH] + jnp.where(high, 0.0, pltpu.roll(part[3 * CH:], 127, 1)) + bias
        stacked.append(jnp.concatenate([even.astype(BF16), odd.astype(BF16)], axis=1))
    fine = jnp.dot(jnp.concatenate(stacked, axis=0), spread_ref[...], preferred_element_type=F32)
    for g in range(2):
        for h in range(2):
            emit(g, h, fine[CH * g:CH * g + CH, 128 * h:128 * h + 128])


def conv_pair(src, w_ref, f, r):
    taps = [
        jnp.concatenate([src(f + t, r + a), src(f + t, r + a + 1)], axis=1)
        for t in range(3) for a in range(3)
    ]
    s = jnp.dot(w_ref[...], jnp.concatenate(taps, axis=0), preferred_element_type=F32)
    lane = lanes_of((CH, 128))
    rows = []
    for h in range(2):
        part = s[:, 128 * h:128 * h + 128]
        left = jnp.where(lane == 0, 0.0, pltpu.roll(part[:CH], 1, 1))
        right = jnp.where(lane == 127, 0.0, pltpu.roll(part[2 * CH:], 127, 1))
        rows.append(left + part[CH:2 * CH] + right)
    return rows


def hidden_frame(act_ref, f, w_ref, bias, gain, hid_ref, to, has_top, has_bottom):
    for pair in range(5):
        rows = conv_pair(lambda i, r: act_ref[i, r], w_ref, f, 2 * pair)
        for h in range(2):
            q = 2 * pair + h
            act = norm_act(rows[h] + bias, gain)
            if q == 0:
                act = jnp.where(has_top, act, 0.0)
            if q == 9:
                act = jnp.where(has_bottom, act, 0.0)
            hid_ref[to, q] = act.astype(BF16)


def decoded_frame(hid_ref, f, w_ref, bias, raw_ref, n, mix_ref, res_ref, to):
    for pair in range(4):
        rows = conv_pair(lambda i, r: hid_ref[i, r], w_ref, f, 2 * pair)
        for h in range(2):
            r = 2 * pair + h
            mix_ref[pl.ds(r, CH, stride=8), :] = raw_ref[n, r].astype(F32) + rows[h] + bias
    res_ref[:, to] = mix_ref[...].reshape(CH, 8, 128).astype(BF16)


def in_image(i, has_top, has_bottom):
    return jnp.logical_and(jnp.logical_or(i > 0, has_top), jnp.logical_or(i < 5, has_bottom))


def first_kernel(flags, x_ref, above_ref, below_ref, wup_ref, spread_ref, w1_ref, cols_ref,
                 act_ref, raw_ref, hid_ref, own_ref):
    has_top, has_bottom = flags[0] > 0, flags[1] > 0
    own_ref[:, :2] = above_ref[...]
    own_ref[:, 2:6] = x_ref[...]
    own_ref[:, 6:] = below_ref[...]

    def row(i, carry):
        ok = in_image(i, has_top, has_bottom)
        for p in range(2):
            def emit(g, h, v, p=p):
                raw_ref[2 * g + h, 2 * i + p] = v.astype(BF16)
                act_ref[2 * g + h, 2 * i + p] = jnp.where(ok, norm_act(v, cols_ref[1]), 0.0).astype(BF16)

            up_tile(lambda d: own_ref[:, i + d].reshape(256, 192), p, None, wup_ref, spread_ref, cols_ref[0], None, emit)
        return carry

    lax.fori_loop(0, 6, row, 0)

    def frame(f, carry):
        hidden_frame(act_ref, f, w1_ref, cols_ref[2], cols_ref[3], hid_ref, f, has_top, has_bottom)
        return carry

    lax.fori_loop(0, 2, frame, 0)


def second_kernel(flags, old_ref, wup_ref, spread_ref, w1_ref, w2_ref, cols_ref, act_ref, raw_ref, new_ref,
                  hid_ref, out_ref, all_act_ref, all_hid_ref, mix_ref, res_ref, sem):
    has_top, has_bottom, has_old = flags[0] > 0, flags[1] > 0, flags[2] > 0
    all_act_ref[2:] = act_ref[:2]
    all_hid_ref[2:] = new_ref[...]

    def row(k, carry):
        i = 2 * k
        for p in range(2):
            def emit(g, h, v, p=p):
                ok = jnp.logical_and(in_image(i + h, has_top, has_bottom), has_old)
                all_act_ref[g, 2 * (i + h) + p] = jnp.where(ok, norm_act(v, cols_ref[1]), 0.0).astype(BF16)

            up_tile(lambda d: old_ref[:, pl.ds(i + d, 2)].reshape(256, 192), p, None, wup_ref, spread_ref, cols_ref[0],
                    None, emit)
        return carry

    lax.fori_loop(0, 3, row, 0)

    def frame(f, carry):
        hidden_frame(all_act_ref, f, w1_ref, cols_ref[2], cols_ref[3], all_hid_ref, f, has_top, has_bottom)
        return carry

    lax.fori_loop(0, 2, frame, 0)
    hid_ref[...] = all_hid_ref[:2]

    def result(f, carry):
        decoded_frame(all_hid_ref, f, w2_ref, cols_ref[4], raw_ref, f, mix_ref, res_ref, f)
        return carry

    lax.fori_loop(0, 2, result, 0)
    copy = pltpu.make_async_copy(res_ref, out_ref.at[:, 2:4], sem)
    copy.start()
    copy.wait()


def third_kernel(flags, w2_ref, cols_ref, raw_ref, past_ref, hid_ref, _, out_ref, all_hid_ref, mix_ref, res_ref, sem):
    all_hid_ref[:2] = jnp.where(flags[2] > 0, past_ref[...], 0)
    all_hid_ref[2:] = hid_ref[...]

    def result(f, carry):
        decoded_frame(all_hid_ref, f, w2_ref, cols_ref[4], raw_ref, f, mix_ref, res_ref, f)
        return carry

    lax.fori_loop(0, 2, result, 0)
    copy = pltpu.make_async_copy(res_ref, out_ref.at[:, :2], sem)
    copy.start()
    copy.wait()


def shape(*dims, dtype=BF16):
    return jax.ShapeDtypeStruct(dims, dtype)


def call(kernel, name, flops, in_specs, out_shape, out_specs, scratch=(), **kw):
    return pl.pallas_call(
        kernel,
        out_shape=out_shape,
        in_specs=in_specs,
        out_specs=out_specs,
        scratch_shapes=list(scratch),
        compiler_params=pltpu.CompilerParams(vmem_limit_bytes=48 << 20),
        cost_estimate=pl.CostEstimate(flops=flops, transcendentals=0, bytes_accessed=4 << 20),
        name=name,
        **kw,
    )


def shards(coarse, up_weight, up_bias, gain_one, conv_one, bias_one, gain_two, conv_two, bias_two):
    tiles, slabs = lax.axis_size("tile"), lax.axis_size("slab")
    later = [(i, i + 1) for i in range(slabs - 1)]
    x = coarse.transpose(1, 2, 3, 0)
    above = lax.ppermute(x[:, 2:], "tile", [(i, i + 1) for i in range(tiles - 1)])
    below = lax.ppermute(x[:, :2], "tile", [(i + 1, i) for i in range(tiles - 1)])
    wup, w1, w2, cols = call(
        prep_kernel, "prep", 1 << 30, [VMEM] * 8,
        (shape(4, 4 * CH, 192), shape(3 * CH, 9 * CH), shape(3 * CH, 9 * CH), shape(5, CH, 128, dtype=F32)), (VMEM,) * 4,
    )(up_weight, conv_one, conv_two, *(v.reshape(1, CH) for v in (up_bias, gain_one, bias_one, gain_two, bias_two)))
    spread = jnp.asarray(spread_matrix(), BF16)
    place, age = lax.axis_index("tile"), lax.axis_index("slab")
    flags = jnp.stack([place, tiles - 1 - place, age]).astype(jnp.int32)
    old = lax.ppermute(jnp.concatenate([above[2:], x[2:], below[2:]], axis=1), "slab", later)
    act, raw, new = call(
        first_kernel, "first", 3 << 30, [SMEM] + [VMEM] * 7,
        (shape(4, 12, CH, 128), shape(4, 12, CH, 128), shape(2, 10, CH, 128)), (VMEM,) * 3,
        [pltpu.VMEM((4, 8, 64, 192), BF16)],
    )(flags, x, above, below, wup, spread, w1, cols)
    past = lax.ppermute(new, "slab", later)
    hid, out = call(
        second_kernel, "second", 3 << 30, [SMEM] + [VMEM] * 9,
        (shape(2, 10, CH, 128), shape(CH, 4, 8, 128)), (VMEM, ANY),
        [pltpu.VMEM((4, 12, CH, 128), BF16), pltpu.VMEM((4, 10, CH, 128), BF16), pltpu.VMEM((CH * 8, 128), F32),
         pltpu.VMEM((CH, 2, 8, 128), BF16), pltpu.SemaphoreType.DMA],
    )(flags, old, wup, spread, w1, w2, cols, act, raw[2:, 2:10], new)
    return call(
        third_kernel, "third", 1 << 30, [SMEM] + [VMEM] * 5 + [ANY],
        shape(CH, 4, 8, 128), ANY,
        [pltpu.VMEM((4, 10, CH, 128), BF16), pltpu.VMEM((CH * 8, 128), F32),
         pltpu.VMEM((CH, 2, 8, 128), BF16), pltpu.SemaphoreType.DMA],
        input_output_aliases={6: 0},
    )(flags, w2, cols, raw[:2, 2:10], past, hid, out)


def solution(mesh):
    return jax.shard_map(
        shards,
        mesh=mesh,
        in_specs=(P(None, "slab", "tile", None), P(), P(), P(), P(), P(), P(), P(), P()),
        out_specs=P(None, "slab", "tile", None),
        check_vma=False,
    )
```

time: 62.1 us -> 46.3 us (0.75)
  the two profiles are of different devices: /device:TPU:56 before, /device:TPU:7 now
where the time goes in v1:
time: 46.3 us; the launch traced here: 46 us
  Pallas kernels  22.3 us (48%)
  starting transfers between devices  14 us (30%)
  waiting for transfers between devices  5.95 us (13%)
  local copies, waits for them, and re-layouts  3.38 us (7%)
    pallas_call x1, Pallas kernels, shards(): call(first_kernel, 'first', 3 << 30, [SMEM] + [VMEM] * 7, (shape(4, 12, C...  9.46 us
    pallas_call x1, Pallas kernels, shards(): call(second_kernel, 'second', 3 << 30, [SMEM] + [VMEM] * 9, (shape(2, 10,...  8.79 us
    ppermute x1, waiting for transfers between devices, shards(): lax.ppermute(x[:, 2:], 'tile', [(i, i + 1) for i in range(tiles - 1)])  5.93 us
    ppermute x1, starting transfers between devices, shards(): lax.ppermute(jnp.concatenate([above[2:], x[2:], below[2:]], axis=1), 'sla...  5.24 us
    ppermute x1, starting transfers between devices, shards(): lax.ppermute(x[:, :2], 'tile', [(i + 1, i) for i in range(tiles - 1)])  4.91 us
    pallas_call x1, Pallas kernels, shards(): call(third_kernel, 'third', 1 << 30, [SMEM] + [VMEM] * 5 + [ANY], shape(C...  3.28 us
    unnamed x20, local copies, waits for them, and re-layouts  2.13 us
    ppermute x1, starting transfers between devices, shards(): lax.ppermute(x[:, 2:], 'tile', [(i, i + 1) for i in range(tiles - 1)])  1.92 us
  transfers between devices with their start and end apart: 4, of which 1 were waited for; matrix products, arithmetic and copies ran while one was open for 0% of the time, Pallas kernels for 41%

profile of v1, /device:TPU:7, one launch (start us, length us, event | category | flops | bytes accessed | tf_op | source)
XLA Modules:
  0.0 46.0 jit_solution(7018548878530086100)
XLA Ops:
  0.0 0.0 copy-start.6
  0.0 0.0 copy-start.1
  0.0 0.0 copy-start.5
  0.0 0.0 copy-start.4
  0.0 1.2 %fusion.1 = (bf16[4,2,64,192]{3,2,1,0:T(8,128)(2,1)S(1)}, bf16[4,2,64,192]{3,2,1,0:T(8,128)(2,1)S(1)}) fusion(bf16[4,4,64,192]{3,2,1,0:T(8,128)(2,1)} %bitcast.9), kind=kLoop, calls=%fused_computation.3 | loop fusion | bytes 786432 | tf_op jit(solution)/shard_map/slice | solution.py:219
  1.2 4.9 %collective-permute-start.1 = (bf16[4,2,64,192]{3,2,1,0:T(8,128)(2,1)S(1)}, bf16[4,2,64,192]{3,2,1,0:T(8,128)(2,1)S(1)}, u32[]{:S(2)}, u32[]{:S(2)}) collective-permute-start(bf16[4,2,64,192]{3,2,1,0:T(8,128)(2,1)S(1)} %get-tuple-element.25), channel_id=1, source_target_pairs={{1,0},{2,1},{3,2},{4,3},{5,4},{6,5},{7,6},{8,7},{9,8},{10,9},{11,1... | collective-permute-start | bytes 589832 | tf_op jit(solution)/shard_map/ppermute | solution.py:219
  6.1 1.9 %collective-permute-start = (bf16[4,2,64,192]{3,2,1,0:T(8,128)(2,1)S(1)}, bf16[4,2,64,192]{3,2,1,0:T(8,128)(2,1)S(1)}, u32[]{:S(2)}, u32[]{:S(2)}) collective-permute-start(bf16[4,2,64,192]{3,2,1,0:T(8,128)(2,1)S(1)} %get-tuple-element.26), channel_id=1, source_target_pairs={{0,1},{1,2},{2,3},{3,4},{4,5},{5,6},{6,7},{7,8},{8,9},{9,10},{10,1... | collective-permute-start | bytes 589832 | tf_op jit(solution)/shard_map/ppermute | solution.py:218
  8.1 0.0 copy-done
  8.1 0.0 copy-done.8
  8.1 0.0 copy-done.7
  8.1 0.0 copy-done.6
  8.1 0.0 copy-done.1
  8.1 0.0 copy-done.5
  8.2 0.0 copy-done.4
  8.2 0.0 copy-start.2
  8.2 1.1 %copy-done.2 = bf16[3,3,96,288]{3,2,1,0:T(8,128)(2,1)S(1)} copy-done((bf16[3,3,96,288]{3,2,1,0:T(8,128)(2,1)S(1)}, bf16[3,3,96,288]{3,2,1,0:T(8,128)(2,1)}, u32[]{:S(2)}) %copy-start.2) | copy-done | bytes 497688
  9.3 1.0 %copy-done.3 = bf16[3,3,96,192]{3,2,1,0:T(8,128)(2,1)S(1)} copy-done((bf16[3,3,96,192]{3,2,1,0:T(8,128)(2,1)S(1)}, bf16[3,3,96,192]{3,2,1,0:T(8,128)(2,1)}, u32[]{:S(2)}) %copy-start.3) | copy-done | bytes 331800
  10.3 0.7 %prep.1 = (bf16[4,384,192]{2,1,0:T(8,128)(2,1)S(1)}, bf16[288,864]{1,0:T(8,128)(2,1)S(1)}, bf16[288,864]{1,0:T(8,128)(2,1)S(1)}, f32[5,96,128]{2,1,0:T(8,128)S(1)}) custom-call(bf16[3,3,96,192]{3,2,1,0:T(8,128)(2,1)S(1)} %copy-done.3, bf16[3,3,96,288]{3,2,1,0:T(8,128)(2,1)S(1)} %copy-done.1, bf16[3,3,96,288]{3,2,1,0:T(8,128)(2,1)S(1)} %copy-done.2, ...), custom_call_target="tpu_custom_call" | custom-call | flops 1073741824 | bytes 4194304 | tf_op jit(solution)/shard_map/prep/pallas_call | solution.py:220
  11.0 0.0 copy-start.9
  11.0 0.1 pad_add_fusion.flags
  11.1 0.0 collective-permute-done.1.below_ref
  11.1 5.9 %collective-permute-done.above_ref = bf16[4,2,64,192]{3,2,1,0:T(8,128)(2,1)S(1)} collective-permute-done((bf16[4,2,64,192]{3,2,1,0:T(8,128)(2,1)S(1)}, bf16[4,2,64,192]{3,2,1,0:T(8,128)(2,1)S(1)}, u32[]{:S(2)}, u32[]{:S(2)}) %collective-permute-start) | collective-permute-done | bytes 196640 | tf_op jit(solution)/shard_map/ppermute | solution.py:218
  17.1 0.1 pad_maximum_fusion
  17.2 5.2 %collective-permute-start.3 = (bf16[2,8,64,192]{3,2,1,0:T(8,128)(2,1)S(1)}, bf16[2,8,64,192]{3,2,1,0:T(8,128)(2,1)S(1)}, u32[]{:S(2)}, u32[]{:S(2)}) collective-permute-start(bf16[2,8,64,192]{3,2,1,0:T(8,128)(2,1)S(1)} %pad_maximum_fusion), channel_id=1, source_target_pairs={{0,16},{16,32},{32,48},{48,64},{64,80},{80,96},{96,112},{1,17},{17... | collective-permute-start | bytes 1179656 | tf_op jit(solution)/shard_map/ppermute | solution.py:227
  22.4 0.0 copy-done.9
  22.4 9.5 %first.1 = (bf16[4,12,96,128]{3,2,1,0:T(8,128)(2,1)S(1)}, bf16[4,12,96,128]{3,2,1,0:T(8,128)(2,1)S(1)}, bf16[2,10,96,128]{3,2,1,0:T(8,128)(2,1)S(1)}) custom-call(s32[3]{0:T(128)S(1)} %pad_add_fusion.flags, bf16[4,4,64,192]{3,2,1,0:T(8,128)(2,1)S(1)} %bitcast.11, bf16[4,2,64,192]{3,2,1,0:T(8,128)(2,1)S(1)} %collective-permute-done.above_ref, ...), custom_call_target="tpu_custom_call" | custom-call | flops 3221225472 | bytes 4194304 | tf_op jit(solution)/shard_map/first/pallas_call | solution.py:228
  31.9 1.9 %collective-permute-start.2 = (bf16[2,10,96,128]{3,2,1,0:T(8,128)(2,1)S(1)}, bf16[2,10,96,128]{3,2,1,0:T(8,128)(2,1)S(1)}, u32[]{:S(2)}, u32[]{:S(2)}) collective-permute-start(bf16[2,10,96,128]{3,2,1,0:T(8,128)(2,1)S(1)} %get-tuple-element.19.new_ref), channel_id=1, source_target_pairs={{0,16},{16,32},{32,48},{48,64},{64,80},{80,96},{96,112},{1,17},{17... | collective-permute-start | bytes 1474568 | tf_op jit(solution)/shard_map/ppermute | solution.py:233
  33.8 0.1 fusion
  33.9 0.0 collective-permute-done.3.old_ref
  33.9 8.8 %second.1 = (bf16[2,10,96,128]{3,2,1,0:T(8,128)(2,1)S(1)}, bf16[96,4,8,128]{3,2,1,0:T(8,128)(2,1)}) custom-call(s32[3]{0:T(128)S(1)} %pad_add_fusion.flags, bf16[2,8,64,192]{3,2,1,0:T(8,128)(2,1)S(1)} %collective-permute-done.3.old_ref, bf16[4,384,192]{2,1,0:T(8,128)(2,1)S(1)} %get-tuple-element.16.wup_ref, bf16[256,256]{1,0:T(8,128)(2,1)S(1)} %copy-done.9, ...), custom_call_target="tpu_custom_call" | custom-call | flops 3221225472 | bytes 4194304 | tf_op jit(solution)/shard_map/second/pallas_call | solution.py:234
  42.7 0.0 collective-permute-done.2.past_ref
  42.7 3.3 %third.1 = bf16[96,4,8,128]{3,2,1,0:T(8,128)(2,1)} custom-call(s32[3]{0:T(128)S(1)} %pad_add_fusion.flags, bf16[288,864]{1,0:T(8,128)(2,1)S(1)} %get-tuple-element.14.w2_ref, f32[5,96,128]{2,1,0:T(8,128)S(1)} %get-tuple-element.15.cols_ref, bf16[2,8,96,128]{3,2,1,0:T(8,128)(2,1)S(1)} %get-tuple-element.24.raw_ref, ...), custom_call_target="tpu_custom_call", output_to_operand_aliasing={{}: (6, {})} | custom-call | flops 1073741824 | bytes 4194304 | tf_op jit(solution)/shard_map/third/pallas_call | solution.py:240
  (7 shorter events, 0.0 us)
Async XLA Ops:
  0.0 8.1 %copy-start = (bf16[192,4,4,64]{0,3,2,1:T(8,128)(2,1)S(1)}, bf16[192,4,4,64]{0,3,2,1:T(8,128)(2,1)}, u32[]{:S(2)}) copy-start(bf16[192,4,4,64]{0,3,2,1:T(8,128)(2,1)} %param.10) | copy-start | bytes 1179652
  0.0 8.1 %copy-start.8 = (f32[96]{0:T(128)S(1)}, f32[96]{0:T(128)}, u32[]{:S(2)}) copy-start(f32[96]{0:T(128)} %param.18) | copy-start | bytes 1156
  0.0 8.1 %copy-start.7 = (f32[96]{0:T(128)S(1)}, f32[96]{0:T(128)}, u32[]{:S(2)}) copy-start(f32[96]{0:T(128)} %param.16) | copy-start | bytes 1156
  0.0 8.1 %copy-start.6 = (f32[96]{0:T(128)S(1)}, f32[96]{0:T(128)}, u32[]{:S(2)}) copy-start(f32[96]{0:T(128)} %param.15) | copy-start | bytes 1156
  0.0 8.1 %copy-start.1 = (bf16[3,3,96,288]{3,2,1,0:T(8,128)(2,1)S(1)}, bf16[3,3,96,288]{3,2,1,0:T(8,128)(2,1)}, u32[]{:S(2)}) copy-start(bf16[3,3,96,288]{3,2,1,0:T(8,128)(2,1)} %one_ref.1) | copy-start | bytes 1492996
  0.0 8.1 %copy-start.5 = (f32[96]{0:T(128)S(1)}, f32[96]{0:T(128)}, u32[]{:S(2)}) copy-start(f32[96]{0:T(128)} %param.13) | copy-start | bytes 1156
  0.0 8.1 %copy-start.4 = (f32[96]{0:T(128)S(1)}, f32[96]{0:T(128)}, u32[]{:S(2)}) copy-start(f32[96]{0:T(128)} %param.12) | copy-start | bytes 1156
  1.2 9.9 %collective-permute-start.1 = (bf16[4,2,64,192]{3,2,1,0:T(8,128)(2,1)S(1)}, bf16[4,2,64,192]{3,2,1,0:T(8,128)(2,1)S(1)}, u32[]{:S(2)}, u32[]{:S(2)}) collective-permute-start(bf16[4,2,64,192]{3,2,1,0:T(8,128)(2,1)S(1)} %get-tuple-element.25), channel_id=1, source_target_pairs={{1,0},{2,1},{3,2},{4,3},{5,4},{6,5},{7,6},{8,7},{9,8},{10,9},{11,1... | collective-permute-start | bytes 589832 | tf_op jit(solution)/shard_map/ppermute | solution.py:219
  6.1 10.9 %collective-permute-start = (bf16[4,2,64,192]{3,2,1,0:T(8,128)(2,1)S(1)}, bf16[4,2,64,192]{3,2,1,0:T(8,128)(2,1)S(1)}, u32[]{:S(2)}, u32[]{:S(2)}) collective-permute-start(bf16[4,2,64,192]{3,2,1,0:T(8,128)(2,1)S(1)} %get-tuple-element.26), channel_id=1, source_target_pairs={{0,1},{1,2},{2,3},{3,4},{4,5},{5,6},{6,7},{7,8},{8,9},{9,10},{10,1... | collective-permute-start | bytes 589832 | tf_op jit(solution)/shard_map/ppermute | solution.py:218
  8.2 1.1 %copy-start.2 = (bf16[3,3,96,288]{3,2,1,0:T(8,128)(2,1)S(1)}, bf16[3,3,96,288]{3,2,1,0:T(8,128)(2,1)}, u32[]{:S(2)}) copy-start(bf16[3,3,96,288]{3,2,1,0:T(8,128)(2,1)} %two_ref.1) | copy-start | bytes 1492996
  9.3 1.0 %copy-start.3 = (bf16[3,3,96,192]{3,2,1,0:T(8,128)(2,1)S(1)}, bf16[3,3,96,192]{3,2,1,0:T(8,128)(2,1)}, u32[]{:S(2)}) copy-start(bf16[3,3,96,192]{3,2,1,0:T(8,128)(2,1)} %up_ref.1) | copy-start | bytes 995332
  11.0 11.4 %copy-start.9 = (bf16[256,256]{1,0:T(8,128)(2,1)S(1)}, bf16[256,256]{1,0:T(8,128)(2,1)}, u32[]{:S(2)}) copy-start(bf16[256,256]{1,0:T(8,128)(2,1)} %constant.13.clone.spread_ref) | copy-start | bytes 393220
  17.2 16.7 %collective-permute-start.3 = (bf16[2,8,64,192]{3,2,1,0:T(8,128)(2,1)S(1)}, bf16[2,8,64,192]{3,2,1,0:T(8,128)(2,1)S(1)}, u32[]{:S(2)}, u32[]{:S(2)}) collective-permute-start(bf16[2,8,64,192]{3,2,1,0:T(8,128)(2,1)S(1)} %pad_maximum_fusion), channel_id=1, source_target_pairs={{0,16},{16,32},{32,48},{48,64},{64,80},{80,96},{96,112},{1,17},{17... | collective-permute-start | bytes 1179656 | tf_op jit(solution)/shard_map/ppermute | solution.py:227
  31.9 10.8 %collective-permute-start.2 = (bf16[2,10,96,128]{3,2,1,0:T(8,128)(2,1)S(1)}, bf16[2,10,96,128]{3,2,1,0:T(8,128)(2,1)S(1)}, u32[]{:S(2)}, u32[]{:S(2)}) collective-permute-start(bf16[2,10,96,128]{3,2,1,0:T(8,128)(2,1)S(1)} %get-tuple-element.19.new_ref), channel_id=1, source_target_pairs={{0,16},{16,32},{32,48},{48,64},{64,80},{80,96},{96,112},{1,17},{17... | collective-permute-start | bytes 1474568 | tf_op jit(solution)/shard_map/ppermute | solution.py:233
